TPU v7x, 256 devices: a whole 4x4x8 slice. The times are simulated.
256 devices in a mesh: section: 8 (over x, core), ep: 32 (over y, z).
Axes of the slice: x: 4, y: 4, z: 8, core: 2. Of those that a mesh axis runs over, the one named last changes fastest.
Arguments:
- hidden_states: bfloat16 [1536, 6144], P('ep'), may hold values from -6 to 6
- route_experts: int32 [1536, 2], P('ep'), may hold values from 0 to 7, all different within a row; in each aligned block of 48 rows (0 to 47, 48 to 95, ...) at most 24 rows name the same one
- route_weights: float32 [1536, 2], P('ep'), may hold values from 0.05 to 1
- gate_weight: bfloat16 [32, 6144, 2048], P('ep', None, 'section'), may hold values from -0.078125 to 0.078125
- up_weight: bfloat16 [32, 6144, 2048], P('ep', None, 'section'), may hold values from -0.078125 to 0.078125
- down_weight: bfloat16 [32, 2048, 6144], P('ep', 'section'), may hold values from -0.0625 to 0.0625
Outputs:
- layer_out: bfloat16 [1536, 6144], P('ep', 'section')
Inputs may be any that keep to these rules, and one draw needn't show every extreme that they name: `route_experts`: each row names two different experts. Among the 48 rows of one ep index no expert is named by more than 24 rows, and in every draw some expert is named by exactly 24 rows of some ep index.
All inputs are finite; a program needn't handle non-finite values.
Results may differ from a plain program's by a relative error of at most 0.015.
Values may be sent and summed in bfloat16 or wider, within the bound.
A program may use at most 128 MiB of HBM per device.

v0:
```python
import jax
import jax.numpy as jnp
from jax import lax
from jax.sharding import PartitionSpec as P

EXPERTS = 8


def cut_along(x, dim, peers):
    before, after = (x.shape[:dim], x.shape[dim + 1 :])
    return jnp.moveaxis(x.reshape(*before, peers, -1, *after), dim, 0)


def sent_and_summed(x, axis, dim):
    peers = lax.axis_size(axis)
    parts = lax.all_to_all(cut_along(x, dim, peers), axis, 0, 0, tiled=True)
    return jnp.sum(parts.astype(jnp.float32), axis=0)


def expert_rows(incoming, gate_weight, up_weight, down_weight):
    sources, slot_count, features = incoming.shape
    stacked = incoming.reshape(sources * slot_count, features)
    gate_value = jnp.dot(stacked, gate_weight[0], preferred_element_type=jnp.float32)
    up_value = jnp.dot(stacked, up_weight[0], preferred_element_type=jnp.float32)
    hidden = (jax.nn.silu(gate_value) * up_value).astype(jnp.bfloat16)
    result = jnp.dot(hidden, down_weight[0], preferred_element_type=jnp.float32).astype(
        jnp.bfloat16
    )
    return result.reshape(sources, slot_count, features)


def on_device(hidden_states, route_experts, route_weights, gate_weight, up_weight, down_weight):
    ep_count = lax.axis_size("ep")
    section_count = lax.axis_size("section")
    tok_rows, features = hidden_states.shape
    members = ep_count // EXPERTS
    capacity = tok_rows // 2
    chosen = route_experts.reshape(-1)
    one_hot = (chosen[:, None] == jnp.arange(EXPERTS, dtype=jnp.int32)[None, :]).astype(jnp.int32)
    earlier = jnp.cumsum(one_hot, axis=0) - one_hot
    slot_index = jnp.sum(earlier * one_hot, axis=1)
    position = (chosen * capacity + slot_index).reshape(tok_rows, 2)
    columns = jnp.arange(EXPERTS * capacity, dtype=jnp.int32)
    matches = position[:, :, None] == columns[None, None, :]
    select = jnp.sum(matches.astype(jnp.int32), axis=1).astype(jnp.bfloat16)
    weighing = jnp.sum(matches.astype(jnp.float32) * route_weights[:, :, None], axis=1)
    packed = jnp.einsum(
        "tj,td->jd", select, hidden_states, preferred_element_type=jnp.float32
    ).astype(jnp.bfloat16)
    outgoing = jnp.repeat(packed.reshape(EXPERTS, capacity, features), members, axis=0)
    slot_share = capacity // section_count
    first_slot = lax.axis_index("section") * slot_share
    own_slots = lax.dynamic_slice_in_dim(outgoing, first_slot, slot_share, 1)
    arrived = lax.all_to_all(own_slots, "ep", split_axis=0, concat_axis=0, tiled=True)
    partials = expert_rows(
        lax.all_gather(arrived, "section", axis=1, tiled=True), gate_weight, up_weight, down_weight
    )
    summed = lax.psum_scatter(
        partials.astype(jnp.float32).astype(jnp.bfloat16),
        "section",
        scatter_dimension=1,
        tiled=True,
    ).astype(jnp.float32)
    returned = lax.all_to_all(
        summed.astype(jnp.bfloat16), "ep", split_axis=0, concat_axis=0, tiled=True
    ).astype(summed.dtype)
    merged = jnp.sum(returned.reshape(EXPERTS, members, slot_share, features), axis=1)
    weigh_part = lax.dynamic_slice_in_dim(
        weighing.reshape(tok_rows, EXPERTS, capacity), first_slot, slot_share, 2
    )
    contribution = jnp.dot(
        weigh_part.reshape(tok_rows, EXPERTS * slot_share),
        merged.reshape(EXPERTS * slot_share, features),
        preferred_element_type=jnp.float32,
    )
    layer_out = sent_and_summed(contribution.astype(jnp.bfloat16), "section", 1)
    return layer_out.astype(jnp.bfloat16)


def solution(mesh):
    return jax.shard_map(
        on_device,
        mesh=mesh,
        in_specs=(
            P("ep", None),
            P("ep", None),
            P("ep", None),
            P("ep", None, "section"),
            P("ep", None, "section"),
            P("ep", "section", None),
        ),
        out_specs=P("ep", "section"),
        check_vma=False,
    )
```

profile of v0, /device:TPU:5, one launch (start us, length us, event | category | flops | bytes accessed | tf_op | source)
XLA Modules:
  0.0 314.7 jit_solution(11855568616730549436)
XLA Ops:
  6.5 0.9 copy.60
  7.5 0.1 eq.28
  7.6 0.1 fusion.21
  7.7 0.1 reduce_window_sum.11
  7.8 0.2 select_reduce_fusion.1
  8.0 0.1 reduce_sum.51
  8.1 0.1 copy.61
  8.2 0.7 multiply_add_fusion
  8.9 0.1 convert_reduce_fusion.1
  9.0 1.9 convolution_convert_fusion.1
  10.8 4.8 %broadcast_in_dim.2 = bf16[8,4,24,6144]{3,2,1,0:T(8,128)(2,1)} broadcast(bf16[8,24,6144]{2,1,0:T(8,128)(2,1)S(1)} %bitcast.41), dimensions={0,2,3} | broadcast | bytes 11796480 | tf_op jit(solution)/shard_map/broadcast_in_dim | solution.py:50
  15.6 4.0 %constant_dynamic-slice_fusion.1 = bf16[32,3,6144]{2,1,0:T(4,128)(2,1)S(1)} fusion(bf16[32,24,6144]{2,1,0:T(8,128)(2,1)} %bitcast.37, s32[]{:T(128)S(6)} %select_n.4), kind=kLoop, calls=%fused_computation.30 | loop fusion | bytes 2359300 | tf_op jit(solution)/shard_map/dynamic_slice | solution.py:53
  19.6 47.5 %all_to_all.15 = bf16[32,3,6144]{2,1,0:T(4,128)(2,1)S(1)} all-to-all(bf16[32,3,6144]{2,1,0:T(4,128)(2,1)S(1)} %constant_dynamic-slice_fusion.1), channel_id=1, replica_groups=mesh['section'=8,'ep'=32] {'ep'}, dimensions={0} | all-to-all | bytes 2359296 | tf_op jit(solution)/shard_map/all_to_all | solution.py:54
  67.1 1.9 copy.64
  68.9 0.0 all-gather.2.cloned.1.call-update
  69.0 0.2 reduce-scatter.2.cloned.1.call-start
  69.2 56.1 %all-gather.2.cloned.1.call-done = bf16[32,24,6144]{2,0,1:T(8,128)(2,1)} async-done(((bf16[32,3,6144]{2,0,1:T(8,128)(2,1)}), bf16[32,24,6144]{2,0,1:T(8,128)(2,1)}) %all-gather.2.cloned.1.call-update) | async-done | bytes 9437200 | tf_op jit(solution)/shard_map/all_gather | solution.py:56
  125.3 12.5 %copy.65 = bf16[32,24,6144]{2,1,0:T(8,128)(2,1)} copy(bf16[32,24,6144]{2,0,1:T(8,128)(2,1)} %all-gather.2.cloned.1.call-done) | data formatting | bytes 18874368 | tf_op jit(solution)/shard_map/all_gather | solution.py:56
  137.8 8.1 %fusion.4 = f32[768,256]{1,0:T(8,128)} fusion(bf16[768,6144]{1,0:T(8,128)(2,1)} %bitcast.38, bf16[1,6144,256]{2,1,0:T(8,128)(2,1)} %param.9), kind=kOutput, calls=%fused_computation.8 | convolution fusion | flops 2415919104 | bytes 13369344 | tf_op jit(solution)/shard_map/dot_general | solution.py:23
  145.9 19.4 %convolution_convert_fusion = bf16[768,6144]{1,0:T(8,128)(2,1)} fusion(bf16[1,256,6144]{2,1,0:T(8,128)(2,1)S(1)} %copy-done, bf16[768,6144]{1,0:T(8,128)(2,1)} %bitcast.39, bf16[1,6144,256]{2,1,0:T(8,128)(2,1)} %param.10, f32[768,256]{1,0:T(8,128)} %fusion.4), kind=kOutput, calls=%fused_computation | convolution fusion | flops 4837736448 | bytes 25952256 | tf_op jit(solution)/shard_map/dot_general | solution.py:26
  165.3 12.5 %copy.66 = bf16[32,24,6144]{2,0,1:T(8,128)(2,1)} copy(bf16[32,24,6144]{2,1,0:T(8,128)(2,1)} %bitcast.40) | data formatting | bytes 18874368 | tf_op jit(solution)/shard_map/reshape | solution.py:29
  177.7 0.0 reduce-scatter.2.cloned.1.call-update
  177.8 59.9 %reduce-scatter.2.cloned.1.call-done = bf16[32,3,6144]{2,0,1:T(8,128)(2,1)} async-done(((bf16[32,24,6144]{2,0,1:T(8,128)(2,1)}), bf16[32,3,6144]{2,0,1:T(8,128)(2,1)}) %reduce-scatter.2.cloned.1.call-update) | async-done | bytes 1179664 | tf_op jit(solution)/shard_map/reduce_scatter | solution.py:58
  237.7 3.4 %copy.67 = bf16[32,3,6144]{2,1,0:T(4,128)(2,1)} copy(bf16[32,3,6144]{2,0,1:T(8,128)(2,1)} %reduce-scatter.2.cloned.1.call-done) | data formatting | bytes 2359296 | tf_op jit(solution)/shard_map/reduce_scatter | solution.py:58
  241.1 9.7 %all-to-all-start.1 = ((bf16[32,3,6144]{2,1,0:T(4,128)(2,1)}), bf16[32,3,6144]{2,1,0:T(4,128)(2,1)}, u32[]{:S(2)}, u32[]{:S(2)}) async-start(bf16[32,3,6144]{2,1,0:T(4,128)(2,1)} %copy.67), calls=%async_computation.2 | async-start | bytes 3145728 | tf_op jit(solution)/shard_map/all_to_all | solution.py:64
  250.8 0.1 select_reduce_fusion
  250.9 0.1 copy.62
  251.0 38.7 %all-to-all-done.1 = bf16[32,3,6144]{2,1,0:T(4,128)(2,1)} async-done(((bf16[32,3,6144]{2,1,0:T(4,128)(2,1)}), bf16[32,3,6144]{2,1,0:T(4,128)(2,1)}, u32[]{:S(2)}, u32[]{:S(2)}) %all-to-all-start.1) | async-done | bytes 1179680 | tf_op jit(solution)/shard_map/all_to_all | solution.py:64
  289.8 2.4 convert_reduce_fusion
  292.1 0.4 fusion
  292.6 13.5 %all_to_all.16 = bf16[8,48,768]{2,1,0:T(8,128)(2,1)} all-to-all(bf16[8,48,768]{2,1,0:T(8,128)(2,1)S(1)} %bitcast.43), channel_id=1, replica_groups=mesh['section'=8,'ep'=32] {'section'}, dimensions={0} | all-to-all | bytes 1179648 | tf_op jit(solution)/shard_map/all_to_all | solution.py:16
  306.1 1.8 reduce_sum.55
  (9 shorter events, 0.1 us)
Async XLA Ops:
  6.5 139.3 %copy-start = (bf16[1,256,6144]{2,1,0:T(8,128)(2,1)S(1)}, bf16[1,256,6144]{2,1,0:T(8,128)(2,1)}, u32[]{:S(2)}) copy-start(bf16[1,256,6144]{2,1,0:T(8,128)(2,1)} %param.11) | copy-start | bytes 9437188
  6.5 118.8 %all-gather.2.cloned.1.call-start = ((), (), s32[]{:S(2)}) async-start(), calls=%async_computation.4 | async-start | bytes 10616832 | tf_op jit(solution)/shard_map/all_gather | solution.py:56
  69.0 168.7 %reduce-scatter.2.cloned.1.call-start = ((), (), s32[]{:S(2)}) async-start(), calls=%async_computation.5 | async-start | bytes 10616832 | tf_op jit(solution)/shard_map/reduce_scatter | solution.py:58
  177.7 73.0 %copy-start.2 = (f32[48,2]{0,1:T(2,128)S(1)}, f32[48,2]{0,1:T(2,128)}, u32[]{:S(2)}) copy-start(f32[48,2]{0,1:T(2,128)} %param.8) | copy-start | bytes 1156
  241.1 48.7 %all-to-all-start.1 = ((bf16[32,3,6144]{2,1,0:T(4,128)(2,1)}), bf16[32,3,6144]{2,1,0:T(4,128)(2,1)}, u32[]{:S(2)}, u32[]{:S(2)}) async-start(bf16[32,3,6144]{2,1,0:T(4,128)(2,1)} %copy.67), calls=%async_computation.2 | async-start | bytes 3145728 | tf_op jit(solution)/shard_map/all_to_all | solution.py:64
  250.8 57.1 %copy-start.1 = (bf16[1,256,6144]{2,1,0:T(8,128)(2,1)S(1)}, bf16[1,256,6144]{2,1,0:T(8,128)(2,1)}, u32[]{:S(2)}) copy-start(bf16[1,256,6144]{2,1,0:T(8,128)(2,1)} %param.11) | copy-start | bytes 9437188
Sparse Core Ops, SparseCore 0:
  69.1 56.1 all-gather.1
  177.9 59.7 reduce-scatter.1
where the time goes:
time: 318 us; the launch traced here: 315 us
  waiting for transfers between devices  155 us (49%)
  blocking collectives  61 us (19%)
  local copies, waits for them, and re-layouts  40.4 us (13%)
  matrix products  29.7 us (9%)
  between operations  13.5 us (4%)
  starting transfers between devices  9.88 us (3%)
  other arithmetic  5.43 us (2%)
    reduce_scatter x1, waiting for transfers between devices, on_device(): lax.psum_scatter(partials.astype(jnp.float32).astype(jnp.bfloat16), 'sect...  59.9 us
    all_gather x1, waiting for transfers between devices, on_device(): lax.all_gather(arrived, 'section', axis=1, tiled=True)  56.1 us
    all_to_all x1, blocking collectives, on_device(): lax.all_to_all(own_slots, 'ep', split_axis=0, concat_axis=0, tiled=True)  47.5 us
    all_to_all x1, waiting for transfers between devices, on_device(): lax.all_to_all(summed.astype(jnp.bfloat16), 'ep', split_axis=0, concat_ax...  38.7 us
    dot_general x1, matrix products, expert_rows(): jnp.dot(hidden, down_weight[0], preferred_element_type=jnp.float32)  19.4 us
    all_to_all x1, blocking collectives, sent_and_summed(): parts = lax.all_to_all(cut_along(x, dim, peers), axis, 0, 0, tiled=True)  13.5 us
    all_gather x1, local copies, waits for them, and re-layouts, on_device(): lax.all_gather(arrived, 'section', axis=1, tiled=True)  12.5 us
    reshape x1, local copies, waits for them, and re-layouts, expert_rows(): return result.reshape(sources, slot_count, features)  12.5 us
  transfers between devices with their start and end apart: 3, of which 3 were waited for; matrix products, arithmetic and copies ran while one was open for 0% of the time, Pallas kernels for 0%

commit v1 on v0

v1 whole, which is shorter than its diff:
```python
import jax
import jax.numpy as jnp
from jax import lax
from jax.experimental import pallas as pl
from jax.experimental.pallas import tpu as pltpu
from jax.sharding import PartitionSpec as P

MESH = pl.DeviceIdType.MESH
BF16 = jnp.bfloat16
F32 = jnp.float32

NX, NY, NZ = 4, 4, 8
SECTIONS = 2 * NX
TOK = 48
CAP = 24
ROWS = NY * CAP
GROUPS = 2
MEMBERS = 4
CHUNKS = NZ
LAST = CHUNKS + 6


def distance(k):
    return jnp.where(k % 2 == 1, (k + 1) // 2, (NZ - k // 2) % NZ)


def kernel(
    hid, experts, weights, wg, wu, wd, out,
    tok, meta, oh, merged, blk, wgu, wdn, xg, part, dbuf, r0, r1, r2, zs, ret, ysend, yret,
    s_loc, s_wd, s_yt, s_ym, s_yr, s_zr, s_x0, s_x1, s_x2, s_pr, s_dr, s_r0, s_r1, s_r2, s_ret,
    s_sa, s_sr, s_sz, s_sy,
):
    feats = tok.shape[-1]
    units = wdn.shape[1]
    s = lax.axis_index("section")
    ep = lax.axis_index("ep")
    c, x = s % 2, s // 2
    y, z = ep // NZ, ep % NZ
    step = 1 - 2 * c
    xa, xb, xo = (x + step + NX) % NX, (x - step + NX) % NX, (x + 2) % NX
    to_a = {"section": 2 * xa + c, "ep": ep}
    to_b = {"section": 2 * xb + c, "ep": ep}
    to_p = {"section": 2 * x + 1 - c, "ep": ep}
    mine, theirs = c * NX, (1 - c) * NX
    me = mine + x

    def at_y(yy):
        return {"section": s, "ep": yy * NZ + z}

    def at_z(zz):
        return {"section": s, "ep": y * NZ + zz}

    def send(src, dst, ssem, rsem, to):
        return pltpu.make_async_remote_copy(
            src_ref=src, dst_ref=dst, send_sem=ssem, recv_sem=rsem, device_id=to, device_id_type=MESH
        )

    def wait(ref, sem):
        pltpu.make_async_copy(ref, ref, sem).wait()

    tok_copy = pltpu.make_async_copy(
        hid.at[:, pl.ds(pl.multiple_of(s * feats, 128), feats)], tok.at[y], s_loc.at[0]
    )
    tok_copy.start()
    g_copy = pltpu.make_async_copy(wg, wgu.at[:, :, pl.ds(0, units)], s_loc.at[1])
    u_copy = pltpu.make_async_copy(wu, wgu.at[:, :, pl.ds(units, units)], s_loc.at[2])
    g_copy.start()
    u_copy.start()
    d_copies = [
        pltpu.make_async_copy(wd.at[:, pl.ds(i * feats, feats)], wdn.at[i], s_wd.at[i])
        for i in range(SECTIONS)
    ]
    for copy in d_copies:
        copy.start()

    meta[y] = jnp.zeros((8, 128), F32)
    meta[y, pl.ds(0, 2), pl.ds(0, TOK)] = weights[...]
    meta[y, pl.ds(2, 2), pl.ds(0, TOK)] = experts[...].astype(F32)

    barrier = pltpu.get_barrier_semaphore()
    peers = [at_y((y + j) % NY) for j in range(1, NY)]
    peers += [at_z((z + d) % NZ) for d in range(1, NZ)]
    peers += [to_a, to_b, to_p]
    for peer in peers:
        pl.semaphore_signal(barrier, inc=1, device_id=peer, device_id_type=MESH)
    pl.semaphore_wait(barrier, len(peers))

    tok_copy.wait()
    for j in range(1, NY):
        to = at_y((y + j) % NY)
        send(meta.at[y], meta.at[y], s_sy.at[0], s_ym.at[j], to).start()
        send(tok.at[y], tok.at[y], s_sy.at[1], s_yt.at[j], to).start()
    for j in range(1, NY):
        wait(meta.at[0], s_ym.at[j])

    lane = lax.broadcasted_iota(jnp.int32, (TOK, 128), 1).astype(F32)
    earlier = (
        lax.broadcasted_iota(jnp.int32, (TOK, TOK), 0) > lax.broadcasted_iota(jnp.int32, (TOK, TOK), 1)
    ).astype(F32).astype(BF16)
    slot_lane = lax.broadcasted_iota(jnp.int32, (TOK, GROUPS * ROWS), 1).astype(F32)
    first_expert = (GROUPS * y).astype(F32)
    for i in range(NY):
        table = meta[i].T[:TOK]
        named = [(table[:, 2 + n : 3 + n] == lane).astype(F32) for n in range(2)]
        before = jnp.dot(earlier, (named[0] + named[1]).astype(BF16), preferred_element_type=F32)
        for n in range(2):
            group = table[:, 2 + n : 3 + n] - first_expert
            place = group * ROWS + i * CAP + jnp.sum(named[n] * before, axis=1, keepdims=True)
            here = (group >= 0.0) & (group < float(GROUPS))
            place = jnp.where(here, place, -1.0)
            oh[n, pl.ds(i * TOK, TOK), :] = (place == slot_lane).astype(F32).astype(BF16)
    for j in range(1, NY):
        wait(tok.at[0], s_yt.at[j])
    packed = lax.dot_general(
        oh[0] + oh[1], tok[...].reshape(NY * TOK, feats), (((0,), (0,)), ((), ())), preferred_element_type=F32
    ).astype(BF16)
    blk[0] = packed[:ROWS]
    blk[1] = packed[ROWS:]
    xg[0, me] = blk[z // MEMBERS]

    for k in range(1, CHUNKS):
        d = (k + 1) // 2 if k % 2 else NZ - k // 2
        zz = (z + d) % NZ
        send(blk.at[zz // MEMBERS], xg.at[k, me], s_sz.at[0], s_zr.at[k], at_z(zz)).start()

    def gather_own(k):
        @pl.when(k > 0)
        def _():
            wait(xg.at[k, me], s_zr.at[k])

        send(xg.at[k, me], xg.at[k, me], s_sa.at[k], s_x0.at[k], to_a).start()
        send(xg.at[k, me], xg.at[k, me], s_sa.at[k], s_x1.at[k], to_b).start()
        send(xg.at[k, me], xg.at[k, me], s_sa.at[k], s_pr.at[k], to_p).start()

    def gather_relay(k):
        src = mine + xb
        wait(xg.at[k, src], s_x0.at[k])
        send(xg.at[k, src], xg.at[k, src], s_sa.at[k], s_x2.at[k], to_a).start()
        send(xg.at[k, src], xg.at[k, src], s_sa.at[k], s_pr.at[k], to_p).start()

    def gather_rest(k):
        wait(xg.at[k, mine + xa], s_x1.at[k])
        send(xg.at[k, mine + xa], xg.at[k, mine + xa], s_sa.at[k], s_pr.at[k], to_p).start()
        wait(xg.at[k, mine + xo], s_x2.at[k])
        send(xg.at[k, mine + xo], xg.at[k, mine + xo], s_sa.at[k], s_pr.at[k], to_p).start()

    def compute(k):
        wait(xg.at[k, pl.ds(0, NX)], s_pr.at[k])
        both = jnp.zeros((ROWS, 2 * units), F32)
        for slot in range(SECTIONS):
            sec = 2 * (slot % NX) + slot // NX
            both = both + jnp.dot(xg[k, slot], wgu[sec], preferred_element_type=F32)
        gate, up = both[:, :units], both[:, units:]
        hidden = (gate / (1.0 + jnp.exp(-gate)) * up).astype(BF16)
        for i in range(NX):
            part[k, theirs + i] = jnp.dot(hidden, wdn[2 * i + 1 - c], preferred_element_type=F32).astype(BF16)
        for i in range(NX):
            part[k, mine + i] = jnp.dot(hidden, wdn[2 * i + c], preferred_element_type=F32).astype(BF16)
            send(part.at[k, theirs + i], dbuf.at[k, i], s_sr.at[k], s_dr.at[k], to_p).start()

    def pair_sum(k, xx):
        return part[k, mine + xx].astype(F32) + dbuf[k, xx].astype(F32)

    def reduce_first(k):
        wait(dbuf.at[k], s_dr.at[k])
        part[k, mine + xo] = pair_sum(k, xo).astype(BF16)
        part[k, mine + xb] = pair_sum(k, xb).astype(BF16)
        send(part.at[k, mine + xo], r0.at[k], s_sr.at[k], s_r0.at[k], to_a).start()
        send(part.at[k, mine + xb], r1.at[k], s_sr.at[k], s_r1.at[k], to_b).start()

    def reduce_relay(k):
        wait(r0.at[k], s_r0.at[k])
        part[k, mine + xa] = (pair_sum(k, xa) + r0[k].astype(F32)).astype(BF16)
        send(part.at[k, mine + xa], r2.at[k], s_sr.at[k], s_r2.at[k], to_a).start()

    def reduce_last(k):
        wait(r1.at[k], s_r1.at[k])
        wait(r2.at[k], s_r2.at[k])
        total = (pair_sum(k, x) + (r1[k].astype(F32) + r2[k].astype(F32))).astype(BF16)
        zs[k] = total

        @pl.when(k == 0)
        def _():
            ret[0] = total

        @pl.when(k > 0)
        def _():
            d = distance(k)
            send(zs.at[k], ret.at[d], s_sz.at[1], s_ret.at[d], at_z((z - d + NZ) % NZ)).start()

    def turn(k, _):
        def stage(f, lag):
            @pl.when((k >= lag) & (k < CHUNKS + lag))
            def _():
                f(k - lag)

        stage(gather_own, 0)
        stage(gather_relay, 1)
        stage(gather_rest, 2)
        stage(reduce_relay, 5)
        stage(reduce_last, 6)
        stage(reduce_first, 4)

        @pl.when(k == 3)
        def _():
            g_copy.wait()
            u_copy.wait()
            for copy in d_copies:
                copy.wait()

        stage(compute, 3)
        return 0

    lax.fori_loop(0, LAST, turn, 0)

    for d in range(1, NZ):
        wait(ret.at[d], s_ret.at[d])
    for g in range(GROUPS):
        total = jnp.zeros((ROWS, feats), F32)
        for m in range(MEMBERS):
            total = total + ret[(MEMBERS * g + m - z + NZ) % NZ].astype(F32)
        merged[pl.ds(g * ROWS, ROWS), :] = total.astype(BF16)
    summed = merged[...]
    for i in range(NY):
        table = meta[i].T[:TOK]
        first = jnp.dot(oh[0, pl.ds(i * TOK, TOK), :], summed, preferred_element_type=F32)
        second = jnp.dot(oh[1, pl.ds(i * TOK, TOK), :], summed, preferred_element_type=F32)
        ysend[i] = (table[:, 0:1] * first + table[:, 1:2] * second).astype(BF16)
    for j in range(1, NY):
        yy = (y + j) % NY
        send(ysend.at[yy], yret.at[j], s_sy.at[2], s_yr.at[j], at_y(yy)).start()
    total = ysend[y].astype(F32)
    for j in range(1, NY):
        wait(yret.at[j], s_yr.at[j])
        total = total + yret[j].astype(F32)
    out[...] = total.astype(BF16)

    for k in range(CHUNKS):
        wait(xg.at[k, pl.ds(0, 7)], s_sa.at[k])
        wait(part.at[k, pl.ds(0, 7)], s_sr.at[k])
    wait(zs.at[pl.ds(0, 7)], s_sz.at[0])
    wait(zs.at[pl.ds(0, 7)], s_sz.at[1])
    wait(meta.at[pl.ds(0, 3)], s_sy.at[0])
    wait(tok.at[pl.ds(0, 3)], s_sy.at[1])
    wait(tok.at[pl.ds(0, 3)], s_sy.at[2])


def on_device(hidden_states, route_experts, route_weights, gate_weight, up_weight, down_weight):
    width = hidden_states.shape[1]
    units = gate_weight.shape[2]
    feats = width // SECTIONS
    dma = pltpu.SemaphoreType.DMA
    block = (ROWS, feats)
    return pl.pallas_call(
        kernel,
        out_shape=jax.ShapeDtypeStruct((TOK, feats), BF16),
        in_specs=[
            pl.BlockSpec(memory_space=pl.ANY),
            pl.BlockSpec(memory_space=pltpu.VMEM),
            pl.BlockSpec(memory_space=pltpu.VMEM),
            *[pl.BlockSpec(memory_space=pl.ANY)] * 3,
        ],
        out_specs=pl.BlockSpec(memory_space=pltpu.VMEM),
        scratch_shapes=[
            pltpu.VMEM((NY, TOK, feats), BF16),
            pltpu.VMEM((NY, 8, 128), F32),
            pltpu.VMEM((2, NY * TOK, GROUPS * ROWS), BF16),
            pltpu.VMEM((GROUPS * ROWS, feats), BF16),
            pltpu.VMEM((GROUPS, *block), BF16),
            pltpu.VMEM((SECTIONS, feats, 2 * units), BF16),
            pltpu.VMEM((SECTIONS, units, feats), BF16),
            pltpu.VMEM((CHUNKS, SECTIONS, *block), BF16),
            pltpu.VMEM((CHUNKS, SECTIONS, *block), BF16),
            pltpu.VMEM((CHUNKS, NX, *block), BF16),
            pltpu.VMEM((CHUNKS, *block), BF16),
            pltpu.VMEM((CHUNKS, *block), BF16),
            pltpu.VMEM((CHUNKS, *block), BF16),
            pltpu.VMEM((CHUNKS, *block), BF16),
            pltpu.VMEM((CHUNKS, *block), BF16),
            pltpu.VMEM((NY, TOK, feats), BF16),
            pltpu.VMEM((NY, TOK, feats), BF16),
            dma((3,)),
            dma((SECTIONS,)),
            *[dma((NY,))] * 3,
            *[dma((CHUNKS,))] * 10,
            dma((CHUNKS,)),
            dma((CHUNKS,)),
            dma((2,)),
            dma((3,)),
        ],
        compiler_params=pltpu.CompilerParams(
            collective_id=0, has_side_effects=True, vmem_limit_bytes=60 * 1024 * 1024
        ),
    )(
        hidden_states,
        route_experts.T,
        route_weights.T,
        gate_weight.reshape(SECTIONS, feats, units),
        up_weight.reshape(SECTIONS, feats, units),
        down_weight.reshape(units, width),
    )


def solution(mesh):
    return jax.shard_map(
        on_device,
        mesh=mesh,
        in_specs=(
            P("ep", None),
            P("ep", None),
            P("ep", None),
            P("ep", None, "section"),
            P("ep", None, "section"),
            P("ep", "section", None),
        ),
        out_specs=P("ep", "section"),
        check_vma=False,
    )
```

time: 318 us -> 125 us (0.39)
  waiting for transfers between devices: 155 us -> 0 us
  Pallas kernels: 0 us -> 123 us
  blocking collectives: 61 us -> 0 us
  local copies, waits for them, and re-layouts: 40.4 us -> 1.52 us
  matrix products: 29.7 us -> 0 us
  between operations: 13.5 us -> 0.01 us
  starting transfers between devices: 9.88 us -> 0 us
  other arithmetic: 5.43 us -> 0 us
    pallas_call x0 -> x1, Pallas kernels: none -> 123 us  [on_device(): pl.pallas_call(kernel, out_shape=jax.ShapeDtypeStruct((TOK, feats), BF16)...]
    all_to_all x2 -> x0, blocking collectives: 61 us -> none  [the longest x1 47.5 us: on_device(): lax.all_to_all(own_slots, 'ep', split_axis=0, concat_axis=0, tiled=True)]
    reduce_scatter x1 -> x0, waiting for transfers between devices: 59.9 us -> none  [on_device(): lax.psum_scatter(partials.astype(jnp.float32).astype(jnp.bfloat16), 'sect...]
    all_gather x1 -> x0, waiting for transfers between devices: 56.1 us -> none  [on_device(): lax.all_gather(arrived, 'section', axis=1, tiled=True)]
    all_to_all x1 -> x0, waiting for transfers between devices: 38.7 us -> none  [on_device(): lax.all_to_all(summed.astype(jnp.bfloat16), 'ep', split_axis=0, concat_ax...]
    dot_general x4 -> x0, matrix products: 29.7 us -> none  [the longest x1 19.4 us: expert_rows(): jnp.dot(hidden, down_weight[0], preferred_element_type=jnp.float32)]
    reshape x2 -> x0, local copies, waits for them, and re-layouts: 12.5 us -> none  [the longest x1 12.5 us: expert_rows(): return result.reshape(sources, slot_count, features)]
    all_gather x1 -> x0, local copies, waits for them, and re-layouts: 12.5 us -> none  [on_device(): lax.all_gather(arrived, 'section', axis=1, tiled=True)]
  transfers between devices with their start and end apart: 3 -> 0, of which waited for: 3 -> 0; matrix products, arithmetic and copies ran while one was open for 0% -> 0% of each run, Pallas kernels for 0% -> 0%
where the time goes in v1:
time: 125 us; the launch traced here: 124 us
  Pallas kernels  123 us (98%)
  local copies, waits for them, and re-layouts  1.52 us (1%)
    pallas_call x1, Pallas kernels, on_device(): pl.pallas_call(kernel, out_shape=jax.ShapeDtypeStruct((TOK, feats), BF16)...  123 us

profile of v1, /device:TPU:5, one launch (start us, length us, event | category | flops | bytes accessed | tf_op | source)
XLA Modules:
  0.0 124.5 jit_solution(6160079651453796706)
XLA Ops:
  0.0 123.0 %shard_map.64 = bf16[48,768]{1,0:T(8,128)(2,1)} custom-call(bf16[48,6144]{1,0:T(8,128)(2,1)} %hid.1, s32[2,48]{1,0:T(2,128)} %bitcast.8, f32[2,48]{1,0:T(2,128)} %bitcast.9, bf16[8,768,256]{2,1,0:T(8,128)(2,1)} %bitcast.5, bf16[8,768,256]{2,1,0:T(8,128)(2,1)} %bitcast.6, bf16[256,6144]{1,0:T(8,128)(2,1)} %bitcast.7), custom_call_target="tpu_custom_call" | custom-call | tf_op jit(solution)/shard_map/pallas_call | solution.py:254
  123.0 1.5 %copy.8 = bf16[48,768]{1,0:T(8,128)(2,1)} copy(bf16[48,768]{1,0:T(8,128)(2,1)} %shard_map.64) | data formatting | bytes 147456

commit v2 on v1

--- a/solution.py
+++ b/solution.py
@@ -17,11 +17,15 @@
 GROUPS = 2
 MEMBERS = 4
 CHUNKS = NZ
-LAST = CHUNKS + 6
+LAST = CHUNKS + 9
 
 
 def distance(k):
     return jnp.where(k % 2 == 1, (k + 1) // 2, (NZ - k // 2) % NZ)
+
+
+def reduce_order(q):
+    return jnp.where(q < 5, q + 3, jnp.where(q == 7, 0, q - 4))
 
 
 def kernel(
@@ -194,13 +198,6 @@
             def _():
                 f(k - lag)
 
-        stage(gather_own, 0)
-        stage(gather_relay, 1)
-        stage(gather_rest, 2)
-        stage(reduce_relay, 5)
-        stage(reduce_last, 6)
-        stage(reduce_first, 4)
-
         @pl.when(k == 3)
         def _():
             g_copy.wait()
@@ -208,7 +205,13 @@
             for copy in d_copies:
                 copy.wait()
 
-        stage(compute, 3)
+        stage(gather_own, 0)
+        stage(gather_relay, 1)
+        stage(gather_rest, 2)
+        stage(lambda q: reduce_first(reduce_order(q)), 7)
+        stage(lambda q: reduce_relay(reduce_order(q)), 8)
+        stage(lambda q: reduce_last(reduce_order(q)), 9)
+        stage(lambda q: compute(reduce_order(q)), 6)
         return 0
 
     lax.fori_loop(0, LAST, turn, 0)

time: 125 us -> 112 us (0.90); the launches traced: 124 us -> 110 us
  Pallas kernels: 123 us -> 108 us
    pallas_call x1, Pallas kernels: 123 us -> 108 us  [on_device(): pl.pallas_call(kernel, out_shape=jax.ShapeDtypeStruct((TOK, feats), BF16)...]
where the time goes in v2:
time: 112 us; the launch traced here: 110 us
  Pallas kernels  108 us (96%)
  local copies, waits for them, and re-layouts  1.52 us (1%)
    pallas_call x1, Pallas kernels, on_device(): pl.pallas_call(kernel, out_shape=jax.ShapeDtypeStruct((TOK, feats), BF16)...  108 us

profile of v2, /device:TPU:5, one launch (start us, length us, event | category | flops | bytes accessed | tf_op | source)
XLA Modules:
  0.0 109.7 jit_solution(483303743120569821)
XLA Ops:
  0.0 108.2 %shard_map.64 = bf16[48,768]{1,0:T(8,128)(2,1)} custom-call(bf16[48,6144]{1,0:T(8,128)(2,1)} %hid.1, s32[2,48]{1,0:T(2,128)} %bitcast.8, f32[2,48]{1,0:T(2,128)} %bitcast.9, bf16[8,768,256]{2,1,0:T(8,128)(2,1)} %bitcast.5, bf16[8,768,256]{2,1,0:T(8,128)(2,1)} %bitcast.6, bf16[256,6144]{1,0:T(8,128)(2,1)} %bitcast.7), custom_call_target="tpu_custom_call" | custom-call | tf_op jit(solution)/shard_map/pallas_call | solution.py:257
  108.2 1.5 %copy.8 = bf16[48,768]{1,0:T(8,128)(2,1)} copy(bf16[48,768]{1,0:T(8,128)(2,1)} %shard_map.64) | data formatting | bytes 147456

commit v3 on v2

--- a/solution.py
+++ b/solution.py
@@ -16,12 +16,17 @@
 ROWS = NY * CAP
 GROUPS = 2
 MEMBERS = 4
+FULL = 2
 CHUNKS = NZ
-LAST = CHUNKS + 9
+LAST = CHUNKS + 8
 
 
 def distance(k):
     return jnp.where(k % 2 == 1, (k + 1) // 2, (NZ - k // 2) % NZ)
+
+
+def gather_order(a):
+    return jnp.where(a == 0, 0, a + FULL)
 
 
 def reduce_order(q):
@@ -31,8 +36,8 @@
 def kernel(
     hid, experts, weights, wg, wu, wd, out,
     tok, meta, oh, merged, blk, wgu, wdn, xg, part, dbuf, r0, r1, r2, zs, ret, ysend, yret,
-    s_loc, s_wd, s_yt, s_ym, s_yr, s_zr, s_x0, s_x1, s_x2, s_pr, s_dr, s_r0, s_r1, s_r2, s_ret,
-    s_sa, s_sr, s_sz, s_sy,
+    s_loc, s_tok, s_wd, s_yt, s_ym, s_yr, s_zr, s_x0, s_x1, s_x2, s_pr, s_dr, s_r0, s_r1, s_r2, s_ret,
+    s_sa, s_sr, s_sz, s_szf, s_sy, s_yf, s_syf,
 ):
     feats = tok.shape[-1]
     units = wdn.shape[1]
@@ -62,12 +67,14 @@
     def wait(ref, sem):
         pltpu.make_async_copy(ref, ref, sem).wait()
 
-    tok_copy = pltpu.make_async_copy(
-        hid.at[:, pl.ds(pl.multiple_of(s * feats, 128), feats)], tok.at[y], s_loc.at[0]
-    )
-    tok_copy.start()
-    g_copy = pltpu.make_async_copy(wg, wgu.at[:, :, pl.ds(0, units)], s_loc.at[1])
-    u_copy = pltpu.make_async_copy(wu, wgu.at[:, :, pl.ds(units, units)], s_loc.at[2])
+    tok_copies = []
+    for i in range(NX):
+        xx = (x + i) % NX
+        start = pl.multiple_of((2 * xx + c) * feats, 128)
+        tok_copies.append(pltpu.make_async_copy(hid.at[:, pl.ds(start, feats)], tok.at[xx, y], s_tok.at[i]))
+        tok_copies[i].start()
+    g_copy = pltpu.make_async_copy(wg, wgu.at[:, :, pl.ds(0, units)], s_loc.at[0])
+    u_copy = pltpu.make_async_copy(wu, wgu.at[:, :, pl.ds(units, units)], s_loc.at[1])
     g_copy.start()
     u_copy.start()
     d_copies = [
@@ -89,11 +96,17 @@
         pl.semaphore_signal(barrier, inc=1, device_id=peer, device_id_type=MESH)
     pl.semaphore_wait(barrier, len(peers))
 
-    tok_copy.wait()
+    for copy in tok_copies:
+        copy.wait()
     for j in range(1, NY):
         to = at_y((y + j) % NY)
         send(meta.at[y], meta.at[y], s_sy.at[0], s_ym.at[j], to).start()
-        send(tok.at[y], tok.at[y], s_sy.at[1], s_yt.at[j], to).start()
+        send(tok.at[x, y], tok.at[x, y], s_sy.at[1], s_yt.at[j], to).start()
+    for i in range(1, NX):
+        xx = (x + i) % NX
+        for j in range(1, NY):
+            to = at_y((y + j) % NY)
+            send(tok.at[xx, y], tok.at[xx, y], s_syf.at[i], s_yf.at[i], to).start()
     for j in range(1, NY):
         wait(meta.at[0], s_ym.at[j])
 
@@ -114,18 +127,38 @@
             place = jnp.where(here, place, -1.0)
             oh[n, pl.ds(i * TOK, TOK), :] = (place == slot_lane).astype(F32).astype(BF16)
     for j in range(1, NY):
-        wait(tok.at[0], s_yt.at[j])
-    packed = lax.dot_general(
-        oh[0] + oh[1], tok[...].reshape(NY * TOK, feats), (((0,), (0,)), ((), ())), preferred_element_type=F32
-    ).astype(BF16)
-    blk[0] = packed[:ROWS]
-    blk[1] = packed[ROWS:]
-    xg[0, me] = blk[z // MEMBERS]
-
-    for k in range(1, CHUNKS):
+        wait(tok.at[0, 0], s_yt.at[j])
+
+    def pack(xx):
+        rows = lax.dot_general(
+            oh[0] + oh[1], tok[xx].reshape(NY * TOK, feats), (((0,), (0,)), ((), ())), preferred_element_type=F32
+        ).astype(BF16)
+        blk[0, xx] = rows[:ROWS]
+        blk[1, xx] = rows[ROWS:]
+
+    pack(x)
+    xg[0, me] = blk[z // MEMBERS, x]
+    for k in range(FULL + 1, CHUNKS):
         d = (k + 1) // 2 if k % 2 else NZ - k // 2
         zz = (z + d) % NZ
-        send(blk.at[zz // MEMBERS], xg.at[k, me], s_sz.at[0], s_zr.at[k], at_z(zz)).start()
+        send(blk.at[zz // MEMBERS, x], xg.at[k, me], s_sz.at[0], s_zr.at[k], at_z(zz)).start()
+
+    def to_nearest(xx):
+        for k in range(1, FULL + 1):
+            zz = (z + (1 if k == 1 else NZ - 1)) % NZ
+            send(blk.at[zz // MEMBERS, xx], xg.at[k, mine + xx], s_szf.at[0], s_zr.at[k], at_z(zz)).start()
+
+    to_nearest(x)
+
+    def spread(i):
+        wait(tok.at[0, pl.ds(0, NY - 1)], s_yf.at[i])
+        xx = (x + i) % NX
+        pack(xx)
+        to_nearest(xx)
+
+    def gather_full(k):
+        wait(xg.at[k, pl.ds(mine, NX)], s_zr.at[k])
+        send(xg.at[k, pl.ds(mine, NX)], xg.at[k, pl.ds(mine, NX)], s_sa.at[k], s_pr.at[k], to_p).start()
 
     def gather_own(k):
         @pl.when(k > 0)
@@ -193,8 +226,8 @@
             send(zs.at[k], ret.at[d], s_sz.at[1], s_ret.at[d], at_z((z - d + NZ) % NZ)).start()
 
     def turn(k, _):
-        def stage(f, lag):
-            @pl.when((k >= lag) & (k < CHUNKS + lag))
+        def stage(f, lag, count=CHUNKS):
+            @pl.when((k >= lag) & (k < count + lag))
             def _():
                 f(k - lag)
 
@@ -205,13 +238,15 @@
             for copy in d_copies:
                 copy.wait()
 
-        stage(gather_own, 0)
-        stage(gather_relay, 1)
-        stage(gather_rest, 2)
-        stage(lambda q: reduce_first(reduce_order(q)), 7)
-        stage(lambda q: reduce_relay(reduce_order(q)), 8)
-        stage(lambda q: reduce_last(reduce_order(q)), 9)
-        stage(lambda q: compute(reduce_order(q)), 6)
+        stage(lambda a: gather_relay(gather_order(a)), 2, CHUNKS - FULL)
+        stage(lambda a: gather_rest(gather_order(a)), 3, CHUNKS - FULL)
+        stage(lambda a: gather_own(gather_order(a)), 0, CHUNKS - FULL)
+        stage(lambda i: spread(i + 1), 1, NX - 1)
+        stage(lambda i: gather_full(i + 1), 8, FULL)
+        stage(lambda q: reduce_first(reduce_order(q)), 6)
+        stage(lambda q: reduce_relay(reduce_order(q)), 7)
+        stage(lambda q: compute(reduce_order(q)), 4)
+        stage(lambda q: reduce_last(reduce_order(q)), 8)
         return 0
 
     lax.fori_loop(0, LAST, turn, 0)
@@ -239,13 +274,16 @@
     out[...] = total.astype(BF16)
 
     for k in range(CHUNKS):
-        wait(xg.at[k, pl.ds(0, 7)], s_sa.at[k])
+        wait(xg.at[k, pl.ds(0, NX if 0 < k <= FULL else 7)], s_sa.at[k])
         wait(part.at[k, pl.ds(0, 7)], s_sr.at[k])
-    wait(zs.at[pl.ds(0, 7)], s_sz.at[0])
+    wait(zs.at[pl.ds(0, CHUNKS - 1 - FULL)], s_sz.at[0])
+    wait(xg.at[0], s_szf.at[0])
+    for i in range(1, NX):
+        wait(tok.at[0, pl.ds(0, 3)], s_syf.at[i])
     wait(zs.at[pl.ds(0, 7)], s_sz.at[1])
     wait(meta.at[pl.ds(0, 3)], s_sy.at[0])
-    wait(tok.at[pl.ds(0, 3)], s_sy.at[1])
-    wait(tok.at[pl.ds(0, 3)], s_sy.at[2])
+    wait(tok.at[0, pl.ds(0, 3)], s_sy.at[1])
+    wait(tok.at[0, pl.ds(0, 3)], s_sy.at[2])
 
 
 def on_device(hidden_states, route_experts, route_weights, gate_weight, up_weight, down_weight):
@@ -265,11 +303,11 @@
         ],
         out_specs=pl.BlockSpec(memory_space=pltpu.VMEM),
         scratch_shapes=[
-            pltpu.VMEM((NY, TOK, feats), BF16),
+            pltpu.VMEM((NX, NY, TOK, feats), BF16),
             pltpu.VMEM((NY, 8, 128), F32),
             pltpu.VMEM((2, NY * TOK, GROUPS * ROWS), BF16),
             pltpu.VMEM((GROUPS * ROWS, feats), BF16),
-            pltpu.VMEM((GROUPS, *block), BF16),
+            pltpu.VMEM((GROUPS, NX, *block), BF16),
             pltpu.VMEM((SECTIONS, feats, 2 * units), BF16),
             pltpu.VMEM((SECTIONS, units, feats), BF16),
             pltpu.VMEM((CHUNKS, SECTIONS, *block), BF16),
@@ -282,14 +320,18 @@
             pltpu.VMEM((CHUNKS, *block), BF16),
             pltpu.VMEM((NY, TOK, feats), BF16),
             pltpu.VMEM((NY, TOK, feats), BF16),
-            dma((3,)),
+            dma((2,)),
+            dma((NX,)),
             dma((SECTIONS,)),
             *[dma((NY,))] * 3,
             *[dma((CHUNKS,))] * 10,
             dma((CHUNKS,)),
             dma((CHUNKS,)),
             dma((2,)),
+            dma((1,)),
             dma((3,)),
+            dma((NX,)),
+            dma((NX,)),
         ],
         compiler_params=pltpu.CompilerParams(
             collective_id=0, has_side_effects=True, vmem_limit_bytes=60 * 1024 * 1024

time: 112 us -> 108 us (0.964); the launches traced: 110 us -> 108 us
  Pallas kernels: 108 us -> 106 us
    pallas_call x1, Pallas kernels: 108 us -> 106 us  [on_device(): pl.pallas_call(kernel, out_shape=jax.ShapeDtypeStruct((TOK, feats), BF16)...]
where the time goes in v3:
time: 108 us
  Pallas kernels  106 us (98%)
  local copies, waits for them, and re-layouts  1.52 us (1%)
    pallas_call x1, Pallas kernels, on_device(): pl.pallas_call(kernel, out_shape=jax.ShapeDtypeStruct((TOK, feats), BF16)...  106 us

profile of v3, /device:TPU:5, one launch (start us, length us, event | category | flops | bytes accessed | tf_op | source)
XLA Modules:
  0.0 107.5 jit_solution(8631802572398649311)
XLA Ops:
  0.0 106.0 %shard_map.64 = bf16[48,768]{1,0:T(8,128)(2,1)} custom-call(bf16[48,6144]{1,0:T(8,128)(2,1)} %hid.1, s32[2,48]{1,0:T(2,128)} %bitcast.8, f32[2,48]{1,0:T(2,128)} %bitcast.9, bf16[8,768,256]{2,1,0:T(8,128)(2,1)} %bitcast.5, bf16[8,768,256]{2,1,0:T(8,128)(2,1)} %bitcast.6, bf16[256,6144]{1,0:T(8,128)(2,1)} %bitcast.7), custom_call_target="tpu_custom_call" | custom-call | tf_op jit(solution)/shard_map/pallas_call | solution.py:295
  106.0 1.5 %copy.8 = bf16[48,768]{1,0:T(8,128)(2,1)} copy(bf16[48,768]{1,0:T(8,128)(2,1)} %shard_map.64) | data formatting | bytes 147456

commit v4 on v3

--- a/solution.py
+++ b/solution.py
@@ -98,7 +98,7 @@
 
     for copy in tok_copies:
         copy.wait()
-    for j in range(1, NY):
+    for j in (2, 1, 3):
         to = at_y((y + j) % NY)
         send(meta.at[y], meta.at[y], s_sy.at[0], s_ym.at[j], to).start()
         send(tok.at[x, y], tok.at[x, y], s_sy.at[1], s_yt.at[j], to).start()
@@ -264,7 +264,7 @@
         first = jnp.dot(oh[0, pl.ds(i * TOK, TOK), :], summed, preferred_element_type=F32)
         second = jnp.dot(oh[1, pl.ds(i * TOK, TOK), :], summed, preferred_element_type=F32)
         ysend[i] = (table[:, 0:1] * first + table[:, 1:2] * second).astype(BF16)
-    for j in range(1, NY):
+    for j in (2, 1, 3):
         yy = (y + j) % NY
         send(ysend.at[yy], yret.at[j], s_sy.at[2], s_yr.at[j], at_y(yy)).start()
     total = ysend[y].astype(F32)

time: 108 us -> 108 us (level)
  no operation moved by 1% of the time
where the time goes in v4:
time: 108 us; the launch traced here: 107 us
  Pallas kernels  105 us (97%)
  local copies, waits for them, and re-layouts  1.52 us (1%)
    pallas_call x1, Pallas kernels, on_device(): pl.pallas_call(kernel, out_shape=jax.ShapeDtypeStruct((TOK, feats), BF16)...  105 us

profile of v4, /device:TPU:5, one launch (start us, length us, event | category | flops | bytes accessed | tf_op | source)
XLA Modules:
  0.0 107.0 jit_solution(3255392776681809708)
XLA Ops:
  0.0 105.5 %shard_map.64 = bf16[48,768]{1,0:T(8,128)(2,1)} custom-call(bf16[48,6144]{1,0:T(8,128)(2,1)} %hid.1, s32[2,48]{1,0:T(2,128)} %bitcast.8, f32[2,48]{1,0:T(2,128)} %bitcast.9, bf16[8,768,256]{2,1,0:T(8,128)(2,1)} %bitcast.5, bf16[8,768,256]{2,1,0:T(8,128)(2,1)} %bitcast.6, bf16[256,6144]{1,0:T(8,128)(2,1)} %bitcast.7), custom_call_target="tpu_custom_call" | custom-call | tf_op jit(solution)/shard_map/pallas_call | solution.py:295
  105.5 1.5 %copy.8 = bf16[48,768]{1,0:T(8,128)(2,1)} copy(bf16[48,768]{1,0:T(8,128)(2,1)} %shard_map.64) | data formatting | bytes 147456
